TPU v7x, 32 devices: a whole 2x2x4 slice. The times are simulated.
32 devices in a mesh: pipe: 4 (over y, core), tensor: 8 (over z, x).
Axes of the slice: x: 2, y: 2, z: 4, core: 2. Of those that a mesh axis runs over, the one named last changes fastest.
Arguments:
- patches: bfloat16 [16384, 1280], P(('pipe', 'tensor')), may hold values from -6 to 6
- attn_gain: float32 [1280], replicated, may hold values from 0.25 to 1.75
- w_qkv: bfloat16 [1280, 3840], P('tensor', 'pipe'), may hold values from -0.1118034 to 0.1118034
- w_out: bfloat16 [1280, 1280], P('tensor', 'pipe'), may hold values from -0.15625 to 0.15625
- merge_gain: float32 [1280], replicated, may hold values from 0.25 to 1.75
- window_ids: int32 [16384], P(('pipe', 'tensor')), may hold values from 0 to 127, as said below
- image_patches: int32 [128], P(('pipe', 'tensor')), may hold values from 0 to 512, as said below
- image_sample: int32 [128], P(('pipe', 'tensor')), may hold values from 0 to 7
Outputs:
- vision_seq: bfloat16 [4, 128, 8, 5120], P('pipe', None, 'tensor')
Inputs may be any that keep to these rules, and one draw needn't show every extreme that they name: `window_ids`: Non-decreasing within each bundle and equal over each 4 consecutive slots; every window lies within one aligned block of 64 slots of a bundle. `image_patches`: multiples of 128; the images of one bundle take at most 512 slots and at least half of them, and in every micro-batch some bundle is full.
All inputs are finite; a program needn't handle non-finite values.
Results may differ from a plain program's by a relative error of at most 0.0053.
Values may be sent and summed in bfloat16 or wider, within the bound.
A program may use at most 64 MiB of HBM per device.

v0:
```python
import math
import jax
import jax.numpy as jnp
from jax import lax
from jax.sharding import PartitionSpec as P

HEADS = 16
WINDOW = 64
SAMPLES = 8
epsilon = 1e-06


def normalize(values, gain_row):
    return (
        values * lax.rsqrt(jnp.mean(values * values, axis=-1, keepdims=True) + epsilon) * gain_row
    )


def token_positions(starts, merged_count, token_count):
    offsets = jnp.cumsum(merged_count) - merged_count
    token_index = jnp.arange(token_count, dtype=jnp.int32)
    inside = (token_index[None, :] >= offsets[:, None]) & (
        token_index[None, :] < (offsets + merged_count)[:, None]
    )
    position = jnp.sum(
        jnp.where(inside, starts[:, None] + token_index[None, :] - offsets[:, None], 0), axis=0
    )
    return jnp.where(jnp.any(inside, axis=0), position, -1)


def body(patches, attn_gain, w_qkv, w_out, merge_gain, window_ids, image_patches, image_sample):
    patch_count, feature_width = patches.shape
    token_count = patch_count // 4
    group_size = lax.axis_size("tensor")
    own_index = lax.axis_index("tensor")
    residual = patches.astype(jnp.float32)
    normed = normalize(residual, attn_gain).astype(jnp.bfloat16)
    qkv_rows = lax.all_gather(w_qkv, "tensor", axis=0, tiled=True)
    qkv = jnp.dot(
        normed,
        lax.all_gather(qkv_rows, "pipe", axis=1, tiled=True),
        preferred_element_type=jnp.float32,
    ).astype(jnp.bfloat16)
    head_width = feature_width // HEADS
    tile_count = patch_count // WINDOW

    def split_heads(block):
        return block.reshape(tile_count, WINDOW, HEADS, head_width)

    queries = split_heads(qkv[:, :feature_width])
    keys_tile = split_heads(qkv[:, feature_width : 2 * feature_width])
    values_tile = split_heads(qkv[:, 2 * feature_width :])
    scores = jnp.einsum(
        "tqhd,tkhd->thqk", queries, keys_tile, preferred_element_type=jnp.float32
    ) * (1.0 / math.sqrt(head_width))
    live_row = jnp.arange(patch_count, dtype=jnp.int32) < jnp.sum(image_patches)
    window_tile = window_ids.reshape(tile_count, WINDOW)
    live_tile = live_row.reshape(tile_count, WINDOW)
    allowed = (window_tile[:, :, None] == window_tile[:, None, :]) & live_tile[:, None, :]
    scores = jnp.where(allowed[:, None, :, :], scores, -1e30)
    row_max = jnp.max(scores, axis=-1, keepdims=True)
    exponent = jnp.exp(scores - row_max)
    weights = (exponent / jnp.sum(exponent, axis=-1, keepdims=True)).astype(jnp.bfloat16)
    context = jnp.einsum(
        "thqk,tkhd->tqhd", weights, values_tile, preferred_element_type=jnp.float32
    ).reshape(patch_count, feature_width)
    context = jnp.where(live_row[:, None], context, 0.0).astype(jnp.bfloat16)
    proj_rows = lax.all_gather(w_out, "tensor", axis=0, tiled=True)
    attended = jnp.dot(
        context,
        lax.all_gather(proj_rows, "pipe", axis=1, tiled=True),
        preferred_element_type=jnp.float32,
    )
    hidden = residual + attended
    merged = (
        normalize(hidden, merge_gain).astype(jnp.bfloat16).reshape(token_count, 4 * feature_width)
    )
    outgoing = merged.reshape(token_count // group_size, group_size, 4 * feature_width)
    merged_count = image_patches // 4
    sample_hot = image_sample[:, None] == jnp.arange(SAMPLES, dtype=jnp.int32)[None, :]
    sample_tally = jnp.sum(jnp.where(sample_hot, merged_count[:, None], 0), axis=0)
    all_tallies = lax.all_gather(sample_tally[None, :], "tensor", axis=0, tiled=True)
    source_ranks = jnp.arange(group_size, dtype=jnp.int32)
    before = jnp.sum(jnp.where((source_ranks < own_index)[:, None], all_tallies, 0), axis=0)
    totals = jnp.sum(all_tallies, axis=0)
    sample_index = jnp.arange(SAMPLES, dtype=jnp.int32)
    sample_base = jnp.sum(
        jnp.where(sample_index[None, :] < sample_index[:, None], totals[None, :], 0), axis=1
    )
    image_order = jnp.arange(image_sample.shape[0], dtype=jnp.int32)
    same_before = (image_sample[None, :] == image_sample[:, None]) & (
        image_order[None, :] < image_order[:, None]
    )
    earlier = jnp.sum(jnp.where(same_before, merged_count[None, :], 0), axis=1)
    starts = jnp.sum(jnp.where(sample_hot, (sample_base + before)[None, :], 0), axis=1) + earlier
    position = token_positions(starts, merged_count, token_count)
    outgoing_position = position.reshape(token_count // group_size, group_size)
    received, received_position = (
        lax.all_to_all(outgoing, "tensor", split_axis=1, concat_axis=0, tiled=True),
        lax.all_to_all(outgoing_position, "tensor", split_axis=1, concat_axis=0, tiled=True),
    )
    dest_rows = received_position.reshape(token_count) // group_size
    placement = (jnp.arange(token_count, dtype=jnp.int32)[:, None] == dest_rows[None, :]).astype(
        jnp.bfloat16
    )
    placed = jnp.dot(
        placement,
        received.reshape(token_count, 4 * feature_width),
        preferred_element_type=jnp.float32,
    )
    return placed.astype(jnp.bfloat16).reshape(1, token_count, 1, 4 * feature_width)


def solution(mesh):
    return jax.shard_map(
        body,
        mesh=mesh,
        in_specs=(
            P(("pipe", "tensor"), None),
            P(),
            P("tensor", "pipe"),
            P("tensor", "pipe"),
            P(),
            P(("pipe", "tensor")),
            P(("pipe", "tensor")),
            P(("pipe", "tensor")),
        ),
        out_specs=P("pipe", None, "tensor", None),
        check_vma=False,
    )
```

profile of v0, /device:TPU:0, one launch (start us, length us, event | category | flops | bytes accessed | tf_op | source)
XLA Modules:
  0.0 223.8 jit_solution(180956799762831658)
XLA Ops:
  6.5 0.7 all-gather.5.cloned.1.call-update
  7.3 59.4 %all-gather.5.cloned.1.call-done = bf16[1280,960]{1,0:T(8,128)(2,1)} async-done(((bf16[160,960]{1,0:T(8,128)(2,1)}), bf16[1280,960]{1,0:T(8,128)(2,1)}) %all-gather.5.cloned.1.call-update) | async-done | bytes 2457616 | tf_op jit(solution)/shard_map/all_gather | solution.py:38
  66.7 4.4 %copy.40 = bf16[1280,960]{0,1:T(8,128)(2,1)} copy(bf16[1280,960]{1,0:T(8,128)(2,1)} %all-gather.5.cloned.1.call-done) | data formatting | bytes 4915200 | tf_op jit(solution)/shard_map/all_gather | solution.py:38
  71.2 33.0 %all_gather.18 = bf16[1280,320]{1,0:T(8,128)(2,1)S(1)} all-gather(bf16[160,320]{1,0:T(8,128)(2,1)S(1)} %copy-done.3), channel_id=1, replica_groups=mesh['pipe'=4,'tensor'=8] {'tensor'}, dimensions={0}, use_global_device_ids=true | all-gather | bytes 921600 | tf_op jit(solution)/shard_map/all_gather | solution.py:68
  104.2 1.3 copy.46
  105.5 0.6 and_select_fusion.1
  106.4 0.6 dynamic-slice
  107.7 0.2 dynamic-update-slice
  108.0 8.6 %all-reduce = s32[64]{0:T(128)S(1)} all-reduce(s32[64]{0:T(128)S(1)} %dynamic-update-slice), channel_id=2, replica_groups=mesh['pipe'=4,'tensor'=8] {'tensor'}, use_global_device_ids=true, to_apply=%add | all-reduce | flops 64 | bytes 512
  117.5 0.7 copy.39
  118.2 4.5 %all-to-all-start = ((s32[16,8,1]{0,2,1:T(1,128)}), s32[16,8,1]{0,2,1:T(1,128)S(1)}, u32[]{:S(2)}, u32[]{:S(2)}) async-start(s32[16,8,1]{0,2,1:T(1,128)} %copy.39), calls=%async_computation | async-start | bytes 8192 | tf_op jit(solution)/shard_map/all_to_all | solution.py:100
  122.8 0.6 iota_compare_fusion.3
  123.5 0.7 add_compare_fusion
  124.1 0.3 fusion.3
  124.7 11.6 %all-gather.7.cloned.1.call-done = bf16[1280,3840]{0,1:T(8,128)(2,1)} async-done(((bf16[1280,960]{0,1:T(8,128)(2,1)}), bf16[1280,3840]{0,1:T(8,128)(2,1)}) %all-gather.7.cloned.1.call-update) | async-done | bytes 9830416 | tf_op jit(solution)/shard_map/all_gather | solution.py:41
  136.3 9.5 %convolution_convert_fusion.1 = bf16[512,3840]{1,0:T(8,128)(2,1)S(1)} fusion(bf16[1280,3840]{0,1:T(8,128)(2,1)} %all-gather.7.cloned.1.call-done, bf16[512,1280]{1,0:T(8,128)(2,1)S(1)} %copy-done.1, f32[1280]{0:T(1024)S(1)} %copy-done.7, f32[512]{0:T(512)S(1)} %add_rsqrt_fusion.1), kind=kOutput, calls=%fused_computation.2 | convolution fusion | flops 5037752320 | bytes 15080448 | tf_op jit(solution)/shard_map/dot_general | solution.py:39
  145.8 1.7 fusion.26
  147.5 4.1 %reshape.158 = bf16[8,64,16,80]{3,2,1,0:T(8,128)(2,1)S(1)} reshape(bf16[512,1280]{1,0:T(8,128)(2,1)} %get-tuple-element.9) | data formatting | bytes 2621440 | tf_op jit(solution)/shard_map/reshape | solution.py:48
  151.6 5.0 %reshape.159 = bf16[8,64,16,80]{3,2,1,0:T(8,128)(2,1)} reshape(bf16[512,1280]{1,0:T(8,128)(2,1)} %get-tuple-element.8) | data formatting | bytes 2621440 | tf_op jit(solution)/shard_map/reshape | solution.py:48
  156.7 4.1 %reshape.157 = bf16[8,64,16,80]{3,2,1,0:T(8,128)(2,1)} reshape(bf16[512,1280]{1,0:T(8,128)(2,1)S(1)} %get-tuple-element.7) | data formatting | bytes 2621440 | tf_op jit(solution)/shard_map/reshape | solution.py:48
  160.8 2.8 %fusion.7 = f32[8,16,64,64]{2,3,1,0:T(8,128)S(1)} fusion(bf16[8,64,16,80]{3,2,1,0:T(8,128)(2,1)} %reshape.159, bf16[8,64,16,80]{3,2,1,0:T(8,128)(2,1)S(1)} %reshape.158), kind=kOutput, calls=%fused_computation.19 | convolution fusion | flops 83886080 | bytes 4718592 | tf_op jit(solution)/shard_map/tqhd,tkhd->thqk/dot_general | solution.py:53
  163.6 1.5 fusion.27
  165.2 1.2 convolution_bitcast_fusion
  166.4 1.4 copy.45
  167.8 3.3 %reshape.160 = bf16[512,1280]{1,0:T(8,128)(2,1)} reshape(bf16[8,64,16,80]{3,2,1,0:T(8,128)(2,1)S(1)} %copy.45) | data formatting | bytes 2621440 | tf_op jit(solution)/shard_map/reshape | solution.py:66
  171.1 4.3 %multiply_reduce_fusion = (f32[512]{0:T(512)S(1)}, f32[512,1280]{1,0:T(8,128)S(1)}) fusion(bf16[1280,1280]{0,1:T(8,128)(2,1)} %all-gather.9.cloned.1.call-done, bf16[512,1280]{1,0:T(8,128)(2,1)} %reshape.160, pred[512]{0:T(512)(128)(4,1)S(1)} %iota_compare_fusion.3, bf16[512,1280]{1,0:T(8,128)(2,1)S(1)} %copy-done.2), kind=kOutput, calls=%fused_computation.15 | convolution fusion | flops 1680997888 | bytes 8522240 | tf_op jit(solution)/shard_map/dot_general | solution.py:69
  175.4 0.3 multiply_convert_fusion
  175.7 0.8 reshape_reshape.3
  176.6 1.8 copy.47
  178.3 5.5 %all-to-all-start.1 = ((bf16[16,8,5120]{2,0,1:T(8,128)(2,1)}), bf16[16,8,5120]{2,0,1:T(8,128)(2,1)S(1)}, u32[]{:S(2)}, u32[]{:S(2)}) async-start(bf16[16,8,5120]{2,0,1:T(8,128)(2,1)} %copy.47), calls=%async_computation.1 | async-start | bytes 2621440 | tf_op jit(solution)/shard_map/all_to_all | solution.py:99
  184.0 31.7 %all-to-all-done.1 = bf16[16,8,5120]{2,0,1:T(8,128)(2,1)S(1)} async-done(((bf16[16,8,5120]{2,0,1:T(8,128)(2,1)}), bf16[16,8,5120]{2,0,1:T(8,128)(2,1)S(1)}, u32[]{:S(2)}, u32[]{:S(2)}) %all-to-all-start.1) | async-done | bytes 1310752 | tf_op jit(solution)/shard_map/all_to_all | solution.py:99
  215.7 1.6 fusion.1
  (50 shorter events, 1.9 us)
Async XLA Ops:
  6.5 60.1 %all-gather.5.cloned.1.call-start = ((), (), s32[]{:S(2)}) async-start(), calls=%async_computation.2 | async-start | bytes 2949120 | tf_op jit(solution)/shard_map/all_gather | solution.py:38
  7.3 63.9 %copy-start.3 = (bf16[160,320]{1,0:T(8,128)(2,1)S(1)}, bf16[160,320]{1,0:T(8,128)(2,1)}, u32[]{:S(2)}) copy-start(bf16[160,320]{1,0:T(8,128)(2,1)} %param.11) | copy-start | bytes 307204
  7.3 129.0 %all-gather.7.cloned.1.call-start = ((), (), s32[]{:S(2)}) async-start(), calls=%async_computation.3 | async-start | bytes 12288000 | tf_op jit(solution)/shard_map/all_gather | solution.py:41
  71.0 34.4 %copy-start.8 = (s32[4]{0:T(128)S(1)}, s32[4]{0:T(128)}, u32[]{:S(2)}) copy-start(s32[4]{0:T(128)} %param.14) | copy-start | bytes 52
  71.0 35.1 %copy-start.6 = (s32[4]{0:T(128)S(1)}, s32[4]{0:T(128)}, u32[]{:S(2)}) copy-start(s32[4]{0:T(128)} %param.15) | copy-start | bytes 52
  71.0 35.4 %copy-start.9 = (u32[32]{0:T(128)S(1)}, u32[32]{0:T(128)}, u32[]{:S(2)}) copy-start(u32[32]{0:T(128)} %constant.61) | copy-start | bytes 388
  71.1 51.7 %copy-start.5 = (s32[512]{0:T(512)S(1)}, s32[512]{0:T(512)}, u32[]{:S(2)}) copy-start(s32[512]{0:T(512)} %param.13) | copy-start | bytes 6148
  71.1 53.1 %copy-start.1 = (bf16[512,1280]{1,0:T(8,128)(2,1)S(1)}, bf16[512,1280]{1,0:T(8,128)(2,1)}, u32[]{:S(2)}) copy-start(bf16[512,1280]{1,0:T(8,128)(2,1)} %param.8) | copy-start | bytes 3932164
  71.1 65.2 %copy-start.7 = (f32[1280]{0:T(1024)S(1)}, f32[1280]{0:T(1024)}, u32[]{:S(2)}) copy-start(f32[1280]{0:T(1024)} %param.9) | copy-start | bytes 15364
  71.1 99.9 %all-gather.9.cloned.1.call-start = ((), (), s32[]{:S(2)}) async-start(), calls=%async_computation.4 | async-start | bytes 4096000 | tf_op jit(solution)/shard_map/all_gather | solution.py:71
  118.2 60.2 %all-to-all-start = ((s32[16,8,1]{0,2,1:T(1,128)}), s32[16,8,1]{0,2,1:T(1,128)S(1)}, u32[]{:S(2)}, u32[]{:S(2)}) async-start(s32[16,8,1]{0,2,1:T(1,128)} %copy.39), calls=%async_computation | async-start | bytes 8192 | tf_op jit(solution)/shard_map/all_to_all | solution.py:100
  163.6 1.6 copy-start
  167.8 3.3 %copy-start.2 = (bf16[512,1280]{1,0:T(8,128)(2,1)S(1)}, bf16[512,1280]{1,0:T(8,128)(2,1)}, u32[]{:S(2)}) copy-start(bf16[512,1280]{1,0:T(8,128)(2,1)} %param.8) | copy-start | bytes 3932164
  171.1 4.4 %copy-start.4 = (f32[1280]{0:T(1024)S(1)}, f32[1280]{0:T(1024)}, u32[]{:S(2)}) copy-start(f32[1280]{0:T(1024)} %param.12) | copy-start | bytes 15364
  178.3 37.3 %all-to-all-start.1 = ((bf16[16,8,5120]{2,0,1:T(8,128)(2,1)}), bf16[16,8,5120]{2,0,1:T(8,128)(2,1)S(1)}, u32[]{:S(2)}, u32[]{:S(2)}) async-start(bf16[16,8,5120]{2,0,1:T(8,128)(2,1)} %copy.47), calls=%async_computation.1 | async-start | bytes 2621440 | tf_op jit(solution)/shard_map/all_to_all | solution.py:99
Sparse Core Ops, SparseCore 0:
  9.5 57.1 all-gather.4
  71.2 65.0 all-gather.6
  137.8 29.2 all-gather.8
where the time goes:
time: 224 us
  waiting for transfers between devices  103 us (46%)
  blocking collectives  41.6 us (19%)
  local copies, waits for them, and re-layouts  29.9 us (13%)
  matrix products  19.4 us (9%)
  between operations  14 us (6%)
  starting transfers between devices  10.1 us (5%)
  other arithmetic  5.32 us (2%)
    all_gather x1, waiting for transfers between devices, body(): qkv_rows = lax.all_gather(w_qkv, 'tensor', axis=0, tiled=True)  59.4 us
    all_gather x1, blocking collectives, body(): proj_rows = lax.all_gather(w_out, 'tensor', axis=0, tiled=True)  33 us
    all_to_all x1, waiting for transfers between devices, body(): lax.all_to_all(outgoing, 'tensor', split_axis=1, concat_axis=0, tiled=True)  31.7 us
    reshape x3, local copies, waits for them, and re-layouts, split_heads(): return block.reshape(tile_count, WINDOW, HEADS, head_width)  13.2 us
    all_gather x1, waiting for transfers between devices, body(): lax.all_gather(qkv_rows, 'pipe', axis=1, tiled=True)  11.6 us
    dot_general x1, matrix products, body(): jnp.dot(normed, lax.all_gather(qkv_rows, 'pipe', axis=1, tiled=True), pre...  9.49 us
    unnamed x1, blocking collectives  8.57 us
    all_to_all x1, starting transfers between devices, body(): lax.all_to_all(outgoing, 'tensor', split_axis=1, concat_axis=0, tiled=True)  5.51 us
  transfers between devices with their start and end apart: 5, of which 3 were waited for; matrix products, arithmetic and copies ran while one was open for 22% of the time, Pallas kernels for 0%

commit v1 on v0

--- a/solution.py
+++ b/solution.py
@@ -38,7 +38,7 @@
     qkv_rows = lax.all_gather(w_qkv, "tensor", axis=0, tiled=True)
     qkv = jnp.dot(
         normed,
-        lax.all_gather(qkv_rows, "pipe", axis=1, tiled=True),
+        jnp.concatenate(lax.all_gather(qkv_rows, "pipe"), axis=1),
         preferred_element_type=jnp.float32,
     ).astype(jnp.bfloat16)
     head_width = feature_width // HEADS

time: 224 us -> 250 us (1.12)
  local copies, waits for them, and re-layouts: 29.9 us -> 50.1 us
  waiting for transfers between devices: 103 us -> 109 us
    all_gather x1, local copies, waits for them, and re-layouts: 4.38 us -> 17.1 us  [body(): lax.all_gather(qkv_rows, 'pipe')]
    reshape x0 -> x1, local copies, waits for them, and re-layouts: none -> 8.88 us  [body(): jnp.concatenate(lax.all_gather(qkv_rows, 'pipe'), axis=1)]
    all_gather x1, waiting for transfers between devices: 11.6 us -> 16.9 us  [body(): lax.all_gather(qkv_rows, 'pipe')]
  transfers between devices with their start and end apart: 5 -> 5, of which waited for: 3 -> 3; matrix products, arithmetic and copies ran while one was open for 22% -> 29% of each run, Pallas kernels for 0% -> 0%
where the time goes in v1:
time: 250 us; the launch traced here: 249 us
  waiting for transfers between devices  109 us (44%)
  local copies, waits for them, and re-layouts  50.1 us (20%)
  blocking collectives  41.6 us (17%)
  matrix products  19.4 us (8%)
  between operations  13.9 us (6%)
  starting transfers between devices  10 us (4%)
  other arithmetic  5.5 us (2%)
    all_gather x1, waiting for transfers between devices, body(): qkv_rows = lax.all_gather(w_qkv, 'tensor', axis=0, tiled=True)  59.4 us
    all_gather x1, blocking collectives, body(): proj_rows = lax.all_gather(w_out, 'tensor', axis=0, tiled=True)  33 us
    all_to_all x1, waiting for transfers between devices, body(): lax.all_to_all(outgoing, 'tensor', split_axis=1, concat_axis=0, tiled=True)  31.7 us
    all_gather x1, local copies, waits for them, and re-layouts, body(): lax.all_gather(qkv_rows, 'pipe')  17.1 us
    all_gather x1, waiting for transfers between devices, body(): lax.all_gather(qkv_rows, 'pipe')  16.9 us
    reshape x3, local copies, waits for them, and re-layouts, split_heads(): return block.reshape(tile_count, WINDOW, HEADS, head_width)  12.3 us
    dot_general x1, matrix products, body(): jnp.dot(normed, jnp.concatenate(lax.all_gather(qkv_rows, 'pipe'), axis=1)...  9.52 us
    reshape x1, local copies, waits for them, and re-layouts, body(): jnp.concatenate(lax.all_gather(qkv_rows, 'pipe'), axis=1)  8.88 us
  transfers between devices with their start and end apart: 5, of which 3 were waited for; matrix products, arithmetic and copies ran while one was open for 29% of the time, Pallas kernels for 0%

profile of v1, /device:TPU:0, one launch (start us, length us, event | category | flops | bytes accessed | tf_op | source)
XLA Modules:
  0.0 249.2 jit_solution(5837964888765551572)
XLA Ops:
  6.5 0.7 all-gather.6.cloned.1.call-update
  7.3 59.4 %all-gather.6.cloned.1.call-done = bf16[1280,960]{1,0:T(8,128)(2,1)} async-done(((bf16[160,960]{1,0:T(8,128)(2,1)}), bf16[1280,960]{1,0:T(8,128)(2,1)}) %all-gather.6.cloned.1.call-update) | async-done | bytes 2457616 | tf_op jit(solution)/shard_map/all_gather | solution.py:38
  66.8 33.0 %all_gather.22 = bf16[1280,320]{1,0:T(8,128)(2,1)S(1)} all-gather(bf16[160,320]{1,0:T(8,128)(2,1)S(1)} %copy-done.3), channel_id=1, replica_groups=mesh['pipe'=4,'tensor'=8] {'tensor'}, dimensions={0}, use_global_device_ids=true | all-gather | bytes 921600 | tf_op jit(solution)/shard_map/all_gather | solution.py:68
  99.8 1.3 copy.58
  101.1 0.6 and_select_fusion.1
  102.2 0.6 dynamic-slice
  103.7 8.6 %all-reduce = s32[64]{0:T(128)S(1)} all-reduce(s32[64]{0:T(128)S(1)} %dynamic-update-slice), channel_id=2, replica_groups=mesh['pipe'=4,'tensor'=8] {'tensor'}, use_global_device_ids=true, to_apply=%add | all-reduce | flops 64 | bytes 512
  113.0 0.7 copy.50
  113.7 4.5 %all-to-all-start = ((s32[16,8,1]{0,2,1:T(1,128)}), s32[16,8,1]{0,2,1:T(1,128)S(1)}, u32[]{:S(2)}, u32[]{:S(2)}) async-start(s32[16,8,1]{0,2,1:T(1,128)} %copy.50), calls=%async_computation | async-start | bytes 8192 | tf_op jit(solution)/shard_map/all_to_all | solution.py:100
  118.3 0.6 iota_compare_fusion.3
  118.9 0.7 add_compare_fusion
  119.6 0.3 fusion.3
  120.2 16.9 %all-gather.10.cloned.1.call-done = bf16[5120,960]{1,0:T(8,128)(2,1)} async-done(((bf16[1280,960]{1,0:T(8,128)(2,1)}), bf16[5120,960]{1,0:T(8,128)(2,1)}) %all-gather.10.cloned.1.call-update) | async-done | bytes 9830416 | tf_op jit(solution)/shard_map/all_gather | solution.py:41
  137.0 17.1 %copy.61 = bf16[4,1280,960]{1,0,2:T(4,128)(2,1)} copy(bf16[4,1280,960]{2,1,0:T(8,128)(2,1)} %bitcast.24) | data formatting | bytes 19660800 | tf_op jit(solution)/shard_map/all_gather | solution.py:41
  154.2 8.9 %copy.52 = bf16[1280,4,960]{0,2,1:T(8,128)(2,1)} copy(bf16[1280,4,960]{0,1,2:T(4,128)(2,1)} %bitcast.23) | data formatting | bytes 19660800 | tf_op jit(solution)/shard_map/reshape | solution.py:41
  163.0 9.5 %convolution_convert_fusion.1 = bf16[512,3840]{1,0:T(8,128)(2,1)S(1)} fusion(bf16[1280,3840]{0,1:T(8,128)(2,1)} %bitcast.25, bf16[512,1280]{1,0:T(8,128)(2,1)S(1)} %copy-done.1, f32[1280]{0:T(1024)S(1)} %copy-done.7, f32[512]{0:T(512)S(1)} %add_rsqrt_fusion.1), kind=kOutput, calls=%fused_computation.2 | convolution fusion | flops 5037752320 | bytes 15080448 | tf_op jit(solution)/shard_map/dot_general | solution.py:39
  172.6 1.3 fusion.26
  173.9 4.1 %reshape.165 = bf16[8,64,16,80]{3,2,1,0:T(8,128)(2,1)} reshape(bf16[512,1280]{1,0:T(8,128)(2,1)S(1)} %get-tuple-element.7) | data formatting | bytes 2621440 | tf_op jit(solution)/shard_map/reshape | solution.py:48
  178.0 4.1 %reshape.167 = bf16[8,64,16,80]{3,2,1,0:T(8,128)(2,1)S(1)} reshape(bf16[512,1280]{1,0:T(8,128)(2,1)} %get-tuple-element.8) | data formatting | bytes 2621440 | tf_op jit(solution)/shard_map/reshape | solution.py:48
  182.1 4.1 %reshape.166 = bf16[8,64,16,80]{3,2,1,0:T(8,128)(2,1)} reshape(bf16[512,1280]{1,0:T(8,128)(2,1)S(1)} %get-tuple-element.9) | data formatting | bytes 2621440 | tf_op jit(solution)/shard_map/reshape | solution.py:48
  186.2 2.8 %fusion.7 = f32[8,16,64,64]{2,3,1,0:T(8,128)S(1)} fusion(bf16[8,64,16,80]{3,2,1,0:T(8,128)(2,1)S(1)} %reshape.167, bf16[8,64,16,80]{3,2,1,0:T(8,128)(2,1)} %reshape.166), kind=kOutput, calls=%fused_computation.19 | convolution fusion | flops 83886080 | bytes 4718592 | tf_op jit(solution)/shard_map/tqhd,tkhd->thqk/dot_general | solution.py:53
  189.0 1.7 fusion.27
  190.7 1.2 convolution_bitcast_fusion
  191.9 1.4 copy.57
  193.3 3.3 %reshape.168 = bf16[512,1280]{1,0:T(8,128)(2,1)} reshape(bf16[8,64,16,80]{3,2,1,0:T(8,128)(2,1)S(1)} %copy.57) | data formatting | bytes 2621440 | tf_op jit(solution)/shard_map/reshape | solution.py:66
  196.6 4.4 %multiply_reduce_fusion = (f32[512]{0:T(512)S(1)}, f32[512,1280]{1,0:T(8,128)S(1)}) fusion(bf16[1280,1280]{0,1:T(8,128)(2,1)} %all-gather.8.cloned.1.call-done, bf16[512,1280]{1,0:T(8,128)(2,1)} %reshape.168, pred[512]{0:T(512)(128)(4,1)S(1)} %iota_compare_fusion.3, bf16[512,1280]{1,0:T(8,128)(2,1)S(1)} %copy-done.2), kind=kOutput, calls=%fused_computation.15 | convolution fusion | flops 1680997888 | bytes 8522240 | tf_op jit(solution)/shard_map/dot_general | solution.py:69
  201.0 0.3 multiply_convert_fusion
  201.3 0.8 reshape_reshape.3
  202.1 1.8 copy.59
  203.9 5.4 %all-to-all-start.1 = ((bf16[16,8,5120]{2,0,1:T(8,128)(2,1)}), bf16[16,8,5120]{2,0,1:T(8,128)(2,1)S(1)}, u32[]{:S(2)}, u32[]{:S(2)}) async-start(bf16[16,8,5120]{2,0,1:T(8,128)(2,1)} %copy.59), calls=%async_computation.1 | async-start | bytes 2621440 | tf_op jit(solution)/shard_map/all_to_all | solution.py:99
  209.4 31.7 %all-to-all-done.1 = bf16[16,8,5120]{2,0,1:T(8,128)(2,1)S(1)} async-done(((bf16[16,8,5120]{2,0,1:T(8,128)(2,1)}), bf16[16,8,5120]{2,0,1:T(8,128)(2,1)S(1)}, u32[]{:S(2)}, u32[]{:S(2)}) %all-to-all-start.1) | async-done | bytes 1310752 | tf_op jit(solution)/shard_map/all_to_all | solution.py:99
  241.1 1.6 fusion.1
  (51 shorter events, 2.0 us)
Async XLA Ops:
  6.5 60.2 %copy-start.3 = (bf16[160,320]{1,0:T(8,128)(2,1)S(1)}, bf16[160,320]{1,0:T(8,128)(2,1)}, u32[]{:S(2)}) copy-start(bf16[160,320]{1,0:T(8,128)(2,1)} %param.11) | copy-start | bytes 307204
  6.5 60.1 %all-gather.6.cloned.1.call-start = ((), (), s32[]{:S(2)}) async-start(), calls=%async_computation.2 | async-start | bytes 2949120 | tf_op jit(solution)/shard_map/all_gather | solution.py:38
  7.3 129.8 %all-gather.10.cloned.1.call-start = ((), (), s32[]{:S(2)}) async-start(), calls=%async_computation.4 | async-start | bytes 13107200 | tf_op jit(solution)/shard_map/all_gather | solution.py:41
  66.7 34.4 %copy-start.8 = (s32[4]{0:T(128)S(1)}, s32[4]{0:T(128)}, u32[]{:S(2)}) copy-start(s32[4]{0:T(128)} %param.14) | copy-start | bytes 52
  66.7 35.0 %copy-start.6 = (s32[4]{0:T(128)S(1)}, s32[4]{0:T(128)}, u32[]{:S(2)}) copy-start(s32[4]{0:T(128)} %param.15) | copy-start | bytes 52
  66.7 35.5 %copy-start.9 = (u32[32]{0:T(128)S(1)}, u32[32]{0:T(128)}, u32[]{:S(2)}) copy-start(u32[32]{0:T(128)} %constant.61) | copy-start | bytes 388
  66.7 51.5 %copy-start.5 = (s32[512]{0:T(512)S(1)}, s32[512]{0:T(512)}, u32[]{:S(2)}) copy-start(s32[512]{0:T(512)} %param.13) | copy-start | bytes 6148
  66.7 52.9 %copy-start.1 = (bf16[512,1280]{1,0:T(8,128)(2,1)S(1)}, bf16[512,1280]{1,0:T(8,128)(2,1)}, u32[]{:S(2)}) copy-start(bf16[512,1280]{1,0:T(8,128)(2,1)} %param.8) | copy-start | bytes 3932164
  66.7 129.9 %all-gather.8.cloned.1.call-start = ((), (), s32[]{:S(2)}) async-start(), calls=%async_computation.3 | async-start | bytes 4096000 | tf_op jit(solution)/shard_map/all_gather | solution.py:71
  113.7 90.2 %all-to-all-start = ((s32[16,8,1]{0,2,1:T(1,128)}), s32[16,8,1]{0,2,1:T(1,128)S(1)}, u32[]{:S(2)}, u32[]{:S(2)}) async-start(s32[16,8,1]{0,2,1:T(1,128)} %copy.50), calls=%async_computation | async-start | bytes 8192 | tf_op jit(solution)/shard_map/all_to_all | solution.py:100
  154.1 8.9 %copy-start.7 = (f32[1280]{0:T(1024)S(1)}, f32[1280]{0:T(1024)}, u32[]{:S(2)}) copy-start(f32[1280]{0:T(1024)} %param.9) | copy-start | bytes 15364
  189.0 1.7 copy-start
  193.3 3.3 %copy-start.2 = (bf16[512,1280]{1,0:T(8,128)(2,1)S(1)}, bf16[512,1280]{1,0:T(8,128)(2,1)}, u32[]{:S(2)}) copy-start(bf16[512,1280]{1,0:T(8,128)(2,1)} %param.8) | copy-start | bytes 3932164
  196.6 4.4 %copy-start.4 = (f32[1280]{0:T(1024)S(1)}, f32[1280]{0:T(1024)}, u32[]{:S(2)}) copy-start(f32[1280]{0:T(1024)} %param.12) | copy-start | bytes 15364
  203.9 37.2 %all-to-all-start.1 = ((bf16[16,8,5120]{2,0,1:T(8,128)(2,1)}), bf16[16,8,5120]{2,0,1:T(8,128)(2,1)S(1)}, u32[]{:S(2)}, u32[]{:S(2)}) async-start(bf16[16,8,5120]{2,0,1:T(8,128)(2,1)} %copy.59), calls=%async_computation.1 | async-start | bytes 2621440 | tf_op jit(solution)/shard_map/all_to_all | solution.py:99
Sparse Core Ops, SparseCore 0:
  9.5 57.1 all-gather.5
  68.2 68.7 all-gather.9
  138.6 29.2 all-gather.7
